TPU v7x, 128 devices: a whole 4x4x4 slice. The times are simulated.
128 devices in a mesh: inter: 2 (over y_hi), intra: 64 (over x, y_lo, z, core).
Axes of the slice: x: 4, y: 4 (y_hi: 2, y_lo: 2; y = y_hi * 2 + y_lo), z: 4, core: 2. Of those that a mesh axis runs over, the one named last changes fastest.
Arguments:
- activations: bfloat16 [262144, 4096], P(('inter', 'intra')), may hold values from -6 to 6
- key_cotangent: bfloat16 [262144, 512], P(('inter', 'intra')), may hold values from -0.046875 to 0.046875
- value_cotangent: bfloat16 [262144, 512], P(('inter', 'intra')), may hold values from -0.046875 to 0.046875
Outputs:
- grad_key: float32 [4096, 512], P('intra')
- grad_value: float32 [4096, 512], P('intra')
All inputs are finite; a program needn't handle non-finite values.
Results may differ from a plain program's by a relative error of at most 0.0029.
Values sent between devices are 32-bit elements; how exact they have to be, the bound alone decides.
A program may use at most 128 MiB of HBM per device.

v0:
```python
import jax
import jax.numpy as jnp
from jax import lax
from jax.sharding import Mesh
from jax.sharding import PartitionSpec as P

INTRA = ("intra_0", "intra_1", "intra_2", "intra_3")
INTER_INTRA = ("inter", "intra_0", "intra_1", "intra_2", "intra_3")


def split_up(value, dim, peers):
    shape = value.shape
    pieces = value.reshape(*shape[:dim], peers, shape[dim] // peers, *shape[dim + 1 :])
    return jnp.moveaxis(pieces, dim, 0)


def summed_rows_2(value, chips, core, dim):
    sizes = (lax.axis_size(chips), lax.axis_size(core))
    pieces = split_up(value, dim, sizes[0] * sizes[1])
    inside = pieces.shape[1:]
    pieces = pieces.reshape(*sizes, *inside).swapaxes(0, 1).reshape(-1, *inside)
    pieces = lax.psum_scatter(pieces, core, scatter_dimension=0, tiled=True)
    return lax.psum_scatter(pieces, chips, scatter_dimension=0, tiled=True)[0]


def copy_for_each(value, axis):
    peers = lax.axis_size(axis)
    return lax.all_to_all(
        jnp.broadcast_to(value[None], (peers, *value.shape)), axis, 0, 0, tiled=True
    )


def of_everyone(value, axis):
    everything = copy_for_each(value, axis)
    return jnp.sum(everything, axis=0)


def term_maker(source, cotangent):
    product = lax.dot_general(
        source, cotangent, (((0,), (0,)), ((), ())), preferred_element_type=jnp.float32
    )
    rounded = lax.optimization_barrier(product.astype(jnp.bfloat16))
    return rounded.astype(jnp.float32)


def local(activations, key_cotangent, value_cotangent):
    cotangent = jnp.concatenate((key_cotangent, value_cotangent), axis=1)
    shard_rows = summed_rows_2(
        term_maker(activations, cotangent), ("intra_0", "intra_1", "intra_2"), "intra_3", 0
    )
    shard_rows = of_everyone(shard_rows, "inter")
    half = cotangent.shape[1] // 2
    return (shard_rows[:, :half], shard_rows[:, half:])


def solution(mesh):
    finer = Mesh(
        mesh.devices.reshape(mesh.shape["inter"], 4, 2, 4, 2),
        ("inter", "intra_0", "intra_1", "intra_2", "intra_3"),
    )
    in_specs = (P(INTER_INTRA, None), P(INTER_INTRA, None), P(INTER_INTRA, None))
    out_specs = (P(INTRA, None), P(INTRA, None))
    return jax.shard_map(local, mesh=finer, in_specs=in_specs, out_specs=out_specs, check_vma=False)
```

profile of v0, /device:TPU:0, one launch (start us, length us, event | category | flops | bytes accessed | tf_op | source)
XLA Modules:
  0.0 291.3 jit_solution(3703138824695536901)
XLA Ops:
  7.2 0.0 reduce-scatter.3.cloned.1.call-start
  7.2 23.2 %convert_bitcast_fusion = bf16[4096,1024]{0,1:T(8,128)(2,1)} fusion(bf16[2048,4096]{1,0:T(8,128)(2,1)} %param.3, bf16[2048,512]{1,0:T(8,128)(2,1)} %param.5, bf16[2048,512]{1,0:T(8,128)(2,1)} %param.4), kind=kOutput, calls=%fused_computation | convolution fusion | flops 17192452096 | bytes 29360128 | tf_op jit(solution)/shard_map/dot_general | solution.py:39
  30.4 12.4 %copy.7 = f32[4096,1024]{1,0:T(8,128)} copy(bf16[4096,1024]{0,1:T(8,128)(2,1)} %convert_bitcast_fusion) | data formatting | bytes 25165824 | tf_op jit(solution)/shard_map/reshape | solution.py:21
  42.8 11.8 %copy.8 = f32[2,32,64,1024]{3,2,1,0:T(8,128)} copy(f32[2,32,64,1024]{3,2,0,1:T(8,128)} %bitcast.9) | data formatting | bytes 33554432 | tf_op jit(solution)/shard_map/reshape | solution.py:21
  54.6 0.0 reduce-scatter.3.cloned.1.call-update
  54.6 0.0 reduce-scatter.5.cloned.1.call-start
  54.7 30.4 %reduce-scatter.3.cloned.1.call-done = f32[32,64,1024]{2,1,0:T(8,128)} async-done(((f32[64,64,1024]{2,1,0:T(8,128)}), f32[32,64,1024]{2,1,0:T(8,128)}) %reduce-scatter.3.cloned.1.call-update) | async-done | bytes 8388624 | tf_op jit(solution)/shard_map/reduce_scatter | solution.py:22
  85.1 0.0 reduce-scatter.5.cloned.1.call-update
  85.1 185.5 %reduce-scatter.5.cloned.1.call-done = f32[1,64,1024]{2,1,0:T(8,128)} async-done(((f32[32,64,1024]{2,1,0:T(8,128)}), f32[1,64,1024]{2,1,0:T(8,128)}) %reduce-scatter.5.cloned.1.call-update) | async-done | bytes 262160 | tf_op jit(solution)/shard_map/reduce_scatter | solution.py:23
  270.6 1.0 broadcast_in_dim.8
  271.6 12.1 %all_to_all.5 = f32[2,64,1024]{2,1,0:T(8,128)S(1)} all-to-all(f32[2,64,1024]{2,1,0:T(8,128)S(1)} %broadcast_in_dim.8), channel_id=1, replica_groups=mesh['inter'=2,'intra_0'=4,'intra_1'=2,'intra_2'=4,'intra_3'=2] {'inter'}, dimensions={0} | all-to-all | bytes 1048576 | tf_op jit(solution)/shard_map/all_to_all | solution.py:28
  283.8 0.7 fusion.4
  (1 shorter events, 0.0 us)
Async XLA Ops:
  7.2 77.9 %reduce-scatter.3.cloned.1.call-start = ((), (), s32[]{:S(2)}) async-start(), calls=%async_computation.3 | async-start | bytes 25165824 | tf_op jit(solution)/shard_map/reduce_scatter | solution.py:22
  54.6 216.0 %reduce-scatter.5.cloned.1.call-start = ((), (), s32[]{:S(2)}) async-start(), calls=%async_computation.4 | async-start | bytes 8650752 | tf_op jit(solution)/shard_map/reduce_scatter | solution.py:23
Sparse Core Ops, SparseCore 0:
  54.7 30.3 reduce-scatter.2
  87.5 183.0 reduce-scatter.4
where the time goes:
time: 292 us; the launch traced here: 291 us
  waiting for transfers between devices  216 us (74%)
  local copies, waits for them, and re-layouts  25.9 us (9%)
  matrix products  23.2 us (8%)
  between operations  14 us (5%)
  blocking collectives  12.1 us (4%)
    reduce_scatter x1, waiting for transfers between devices, summed_rows_2(): return lax.psum_scatter(pieces, chips, scatter_dimension=0, tiled=True)[0]  185 us
    reduce_scatter x1, waiting for transfers between devices, summed_rows_2(): pieces = lax.psum_scatter(pieces, core, scatter_dimension=0, tiled=True)  30.4 us
    reshape x2, local copies, waits for them, and re-layouts, summed_rows_2(): pieces = pieces.reshape(*sizes, *inside).swapaxes(0, 1).reshape(-1, *inside)  24.2 us
    dot_general x1, matrix products, term_maker(): lax.dot_general(source, cotangent, (((0,), (0,)), ((), ())), preferred_el...  23.2 us
    all_to_all x1, blocking collectives, copy_for_each(): lax.all_to_all(jnp.broadcast_to(value[None], (peers, *value.shape)), axis...  12.1 us
  transfers between devices with their start and end apart: 2, of which 2 were waited for; matrix products, arithmetic and copies ran while one was open for 0% of the time, Pallas kernels for 0%

commit v1 on v0

v1 whole, which is shorter than its diff:
```python
import functools

import jax
import jax.numpy as jnp
from jax import lax
from jax.experimental import pallas as pl
from jax.experimental.pallas import tpu as pltpu
from jax.sharding import Mesh
from jax.sharding import PartitionSpec as P

MESH = pl.DeviceIdType.MESH
F32 = jnp.float32
AXES = ("inter", "x", "ylo", "z", "core")
INTRA = ("x", "ylo", "z", "core")

ORDER = {"x": (2, 1, 3, 0), "y": (1, 2, 3, 0), "z": (1, 2, 3, 0)}
SIZES = (48, 40, 40, 40, 48, 40)
KEEP = 3
LAG = 4


def flip(r, k):
    if k == 0:
        return r
    if k == 1:
        return r + 1 - 2 * (r % 2)
    if k == 2:
        return (r + 2) % 4
    return 3 - r


def colours():
    result, off = [], 0
    index = 0
    for order in ("xyz", "yzx", "zxy"):
        for p1, p2 in ((1, 3), (3, 1)):
            result.append((index, order, p1, p2, pl.ds(off, SIZES[index])))
            off += SIZES[index]
            index += 1
    return result


def slot(axis, k):
    return ORDER[axis].index(k)


def pair_start(p1):
    return 0 if p1 == 1 else 1


def pair_item(p1, keep):
    first_is_keep = p1 == 1
    return 0 if first_is_keep == keep else 1


def kernel(
    a_hbm, k_hbm, v_hbm, out_k, out_v,
    abuf, cst, ct, acc, dsend, drecv, r1, r2, r3, r4, r5, r6, fin, obuf,
    a_sem, c_sem, ds_sem, dr_sem, s1s, s1r, s2s, s2r, s3s, s3r, s4s, s4r, s5s, s5r, s6s, s6r, fs_sem, fr_sem,
):
    tok = a_hbm.shape[0]
    x, z = lax.axis_index("x"), lax.axis_index("z")
    yhi, ylo = lax.axis_index("inter"), lax.axis_index("ylo")
    core = lax.axis_index("core")
    y = 2 * yhi + ylo
    cols = colours()

    def peer(axis, k):
        if axis == "x":
            return {"x": flip(x, k)}
        if axis == "z":
            return {"z": flip(z, k)}
        to = flip(y, k)
        return {"inter": to // 2, "ylo": to % 2}

    other_core = {"core": 1 - core}
    far = {"inter": 1 - yhi}
    far_other = {"inter": 1 - yhi, "core": 1 - core}

    barrier = pltpu.get_barrier_semaphore()
    peers = [other_core, far, far_other] + [peer(axis, k) for axis in "xyz" for k in (1, 3)]
    for device in peers:
        pl.semaphore_signal(barrier, inc=1, device_id=device, device_id_type=MESH)

    def c_copy(which, hrel):
        src = (k_hbm, v_hbm)[which]
        rel = core if which == 0 else 1 - core
        half = (yhi + hrel) % 2
        return pltpu.make_async_copy(
            src.at[:, pl.ds(pl.multiple_of(half * 256, 256), 256)], cst.at[rel, hrel], c_sem.at[which, hrel]
        )

    for which in (0, 1):
        for hrel in (0, 1):
            c_copy(which, hrel).start()

    def a_copy(u, lrel, column):
        return pltpu.make_async_copy(
            a_hbm.at[:, pl.ds(column, 128)], abuf.at[u, :, pl.ds(lrel * 128, 128)], a_sem.at[u, lrel]
        )

    for sx in range(4):
        for sz in range(4):
            for lrel in (0, 1):
                tx, tz = flip(x, ORDER["x"][sx]), flip(z, ORDER["z"][sz])
                tl = (ylo + lrel) % 2
                column = pl.multiple_of(((tx * 2 + tl) * 4 + tz) * 128, 128)
                a_copy(sx * 4 + sz, lrel, column).start()

    for which in (0, 1):
        for hrel in (0, 1):
            c_copy(which, hrel).wait()
    for rel in (1, 0):
        for hrel in (0, 1):
            ct[rel, pl.ds(hrel * 256, 256), :] = cst[rel, hrel].T

    pl.semaphore_wait(barrier, len(peers))

    def remote(src, dst, send, recv, device):
        return pltpu.make_async_remote_copy(
            src_ref=src, dst_ref=dst, send_sem=send, recv_sem=recv, device_id=device, device_id_type=MESH
        )

    def d2d(v):
        return remote(dsend.at[v], drecv.at[v], ds_sem.at[v], dr_sem.at[v], other_core)

    def send1(c, v, sx, sz, i, j):
        index, order, p1, p2, rows = c
        axis = order[0]
        if axis == "y":
            src = acc.at[sx, sz, pl.ds(pair_start(p1), 2), rows]
            return remote(src, r1.at[pl.ds(v * 2, 2), rows], s1s.at[index, v], s1r.at[index, v], peer(axis, p1))
        n = i * 4 + j
        return remote(
            acc.at[sx, sz, :, rows], r1.at[pl.ds(n * 4, 4), rows], s1s.at[index, n], s1r.at[index, n], peer(axis, p1)
        )

    def send2(c, sx, sz, n):
        index, order, p1, p2, rows = c
        axis = order[0]
        if axis == "y":
            src = acc.at[sx, sz, slot("y", p2), rows]
            return remote(src, r2.at[n, rows], s2s.at[index, n], s2r.at[index, n], peer(axis, p2))
        return remote(
            acc.at[sx, sz, :, rows], r2.at[pl.ds(n * 4, 4), rows], s2s.at[index, n], s2r.at[index, n], peer(axis, p2)
        )

    def process(v):
        sx, sz = v // 4, v % 4
        d2d(v).wait_recv()
        acc[sx, sz] = acc[sx, sz] + drecv[v]
        for c in cols:
            index, order, p1, p2, rows = c
            if order[0] == "y":
                send1(c, v, sx, sz, 0, 0).start()
            else:
                axis = order[0]
                mine, rest = (sx, sz) if axis == "x" else (sz, sx)
                for i, k in ((0, 2), (1, p1)):

                    @pl.when(mine == slot(axis, k))
                    def _(c=c, i=i, rest=rest):
                        send1(c, v, sx, sz, i, rest).start()

    def process2(v):
        sx, sz = v // 4, v % 4
        for c in cols:
            index, order, p1, p2, rows = c
            axis = order[0]
            if axis == "y":
                send1(c, v, sx, sz, 0, 0).wait_recv()
                on = slot("y", p2)
                acc[sx, sz, on, rows] = acc[sx, sz, on, rows] + r1[v * 2 + pair_item(p1, False), rows]
                acc[sx, sz, KEEP, rows] = acc[sx, sz, KEEP, rows] + r1[v * 2 + pair_item(p1, True), rows]
                send2(c, sx, sz, v).start()
            elif axis == "x":

                @pl.when(sx == slot("x", p2))
                def _(c=c, index=index, rows=rows):
                    send1(c, v, sx, sz, 0, sz).wait_recv()
                    acc[sx, sz, :, rows] = acc[sx, sz, :, rows] + r1[pl.ds(sz * 4, 4), rows]
                    send2(c, sx, sz, sz).start()
            else:

                @pl.when(sz == 3)
                def _(c=c, p2=p2, rows=rows):
                    on = slot("z", p2)
                    send1(c, v, sx, on, 0, sx).wait_recv()
                    acc[sx, on, :, rows] = acc[sx, on, :, rows] + r1[pl.ds(sx * 4, 4), rows]
                    send2(c, sx, on, sx).start()

    def step(u, carry):
        @pl.when(u < 16)
        def _():
            sx, sz = u // 4, u % 4
            a_copy(u, 0, 0).wait()
            a_copy(u, 1, 0).wait()
            for rel in (1, 0):
                product = jnp.dot(ct[rel], abuf[u], preferred_element_type=F32)
                for hrel in (0, 1):
                    for lrel in (0, 1):
                        block = product[hrel * 256 : hrel * 256 + 256, lrel * 128 : lrel * 128 + 128]
                        target = slot("y", 2 * hrel + lrel)
                        if rel == 1:
                            dsend[u, target] = block
                        else:
                            acc[sx, sz, target] = block
                if rel == 1:
                    d2d(u).start()

        @pl.when((u >= 1) & (u <= 16))
        def _():
            process(u - 1)

        @pl.when(u >= LAG)
        def _():
            process2(u - LAG)

        return carry

    lax.fori_loop(0, 16 + LAG, step, 0)

    xs, ys, zs = cols[0:2], cols[2:4], cols[4:6]

    def x_send3(c, sz):
        index, _, p1, _, rows = c
        return remote(
            acc.at[3, sz, pl.ds(pair_start(p1), 2), rows], r3.at[pl.ds(sz * 2, 2), rows],
            s3s.at[index, sz], s3r.at[index, sz], peer("y", p1),
        )

    def y_send3(c, sx):
        index, _, p1, _, rows = c
        return remote(
            acc.at[sx, pl.ds(pair_start(p1), 2), KEEP, rows], r3.at[pl.ds(sx * 2, 2), rows],
            s3s.at[index, sx], s3r.at[index, sx], peer("z", p1),
        )

    def z_send3(c, i):
        index, _, p1, _, rows = c
        sx = slot("x", (2, p1)[i])
        return remote(
            acc.at[sx, KEEP, :, rows], r3.at[pl.ds(i * 4, 4), rows],
            s3s.at[index, i], s3r.at[index, i], peer("x", p1),
        )

    for sz in range(4):
        for c in xs:
            rows = c[4]
            send1(c, 0, 0, 0, 1, sz).wait_recv()
            send2(c, 0, 0, sz).wait_recv()
            acc[3, sz, :, rows] = acc[3, sz, :, rows] + (r1[pl.ds(16 + sz * 4, 4), rows] + r2[pl.ds(sz * 4, 4), rows])
            x_send3(c, sz).start()

    for sx in range(4):
        for c in zs:
            _, _, p1, _, rows = c
            send1(c, 0, 0, 0, 1, sx).wait_recv()
            send2(c, 0, 0, sx).wait_recv()
            acc[sx, 3, :, rows] = acc[sx, 3, :, rows] + (r1[pl.ds(16 + sx * 4, 4), rows] + r2[pl.ds(sx * 4, 4), rows])
            for i in (0, 1):
                if sx == slot("x", (2, p1)[i]):
                    z_send3(c, i).start()
        for c in ys:
            rows = c[4]
            for sz in range(4):
                send2(c, 0, 0, sx * 4 + sz).wait_recv()
            acc[sx, :, KEEP, rows] = acc[sx, :, KEEP, rows] + r2[pl.ds(sx * 4, 4), rows]
            y_send3(c, sx).start()

    def x_send4(c):
        index, _, _, p2, rows = c
        return remote(acc.at[3, :, slot("y", p2), rows], r4.at[:, rows], s4s.at[index], s4r.at[index], peer("y", p2))

    def y_send4(c):
        index, _, _, p2, rows = c
        return remote(acc.at[:, slot("z", p2), KEEP, rows], r4.at[:, rows], s4s.at[index], s4r.at[index], peer("z", p2))

    def z_send4(c):
        index, _, _, p2, rows = c
        return remote(acc.at[slot("x", p2), KEEP, :, rows], r4.at[:, rows], s4s.at[index], s4r.at[index], peer("x", p2))

    for c in xs:
        _, _, p1, p2, rows = c
        on = slot("y", p2)
        for sz in range(4):
            x_send3(c, sz).wait_recv()
            acc[3, sz, on, rows] = acc[3, sz, on, rows] + r3[sz * 2 + pair_item(p1, False), rows]
            acc[3, sz, KEEP, rows] = acc[3, sz, KEEP, rows] + r3[sz * 2 + pair_item(p1, True), rows]
        x_send4(c).start()
    for c in zs:
        _, _, p1, p2, rows = c
        on = slot("x", p2)
        z_send3(c, 0).wait_recv()
        acc[on, KEEP, :, rows] = acc[on, KEEP, :, rows] + r3[pl.ds(0, 4), rows]
        z_send4(c).start()
    for c in ys:
        _, _, p1, p2, rows = c
        on = slot("z", p2)
        for sx in range(4):
            y_send3(c, sx).wait_recv()
            acc[sx, on, KEEP, rows] = acc[sx, on, KEEP, rows] + r3[sx * 2 + pair_item(p1, False), rows]
            acc[sx, 3, KEEP, rows] = acc[sx, 3, KEEP, rows] + r3[sx * 2 + pair_item(p1, True), rows]
        y_send4(c).start()

    def x_send5(c):
        index, _, p1, _, rows = c
        return remote(
            acc.at[3, pl.ds(pair_start(p1), 2), KEEP, rows], r5.at[:, rows], s5s.at[index, 0], s5r.at[index, 0], peer("z", p1)
        )

    def z_send5(c):
        index, _, p1, _, rows = c
        return remote(
            acc.at[3, KEEP, pl.ds(pair_start(p1), 2), rows], r5.at[:, rows], s5s.at[index, 0], s5r.at[index, 0], peer("y", p1)
        )

    def y_send5(c, i):
        index, _, p1, _, rows = c
        return remote(
            acc.at[slot("x", (2, p1)[i]), KEEP, KEEP, rows], r5.at[i, rows], s5s.at[index, i], s5r.at[index, i], peer("x", p1)
        )

    for c in xs:
        rows = c[4]
        x_send4(c).wait_recv()
        acc[3, :, KEEP, rows] = acc[3, :, KEEP, rows] + r4[:, rows]
        x_send5(c).start()
    for c in zs:
        _, _, p1, _, rows = c
        z_send3(c, 1).wait_recv()
        z_send4(c).wait_recv()
        acc[3, KEEP, :, rows] = acc[3, KEEP, :, rows] + (r3[pl.ds(4, 4), rows] + r4[:, rows])
        z_send5(c).start()
    for c in ys:
        rows = c[4]
        y_send4(c).wait_recv()
        acc[:, 3, KEEP, rows] = acc[:, 3, KEEP, rows] + r4[:, rows]
        for i in (0, 1):
            y_send5(c, i).start()

    def last(c, axis):
        index, _, _, p2, rows = c
        on = slot(axis, p2)
        src = {"x": acc.at[on, KEEP, KEEP, rows], "y": acc.at[3, KEEP, on, rows], "z": acc.at[3, on, KEEP, rows]}[axis]
        return remote(src, r6.at[rows], s6s.at[index], s6r.at[index], peer(axis, p2))

    for group, axis in ((xs, "z"), (zs, "y"), (ys, "x")):
        for c in group:
            _, _, p1, p2, rows = c
            on = slot(axis, p2)
            if axis == "x":
                y_send5(c, 0).wait_recv()
                y_send5(c, 1).wait_recv()
                onward, kept = r5[0, rows], r5[1, rows]
                acc[on, KEEP, KEEP, rows] = acc[on, KEEP, KEEP, rows] + onward
            else:
                (x_send5 if axis == "z" else z_send5)(c).wait_recv()
                onward, kept = r5[pair_item(p1, False), rows], r5[pair_item(p1, True), rows]
                if axis == "z":
                    acc[3, on, KEEP, rows] = acc[3, on, KEEP, rows] + onward
                else:
                    acc[3, KEEP, on, rows] = acc[3, KEEP, on, rows] + onward
            last(c, axis).start()
            acc[3, KEEP, KEEP, rows] = acc[3, KEEP, KEEP, rows] + kept

    for group, axis in ((xs, "z"), (zs, "y"), (ys, "x")):
        for c in group:
            last(c, axis).wait_recv()

    fin[...] = (acc[3, KEEP, KEEP] + r6[...]).T
    place = pl.ds(pl.multiple_of(yhi * 256, 256), 256)

    def spread(n, to_core, device):
        return remote(
            fin.at[pl.ds(to_core * 64, 64)], obuf.at[core, :, place], fs_sem.at[n], fr_sem.at[n], device
        )

    sends = (
        spread(0, core, far), spread(1, 1 - core, far_other), spread(2, 1 - core, other_core),
    )
    for copy in sends:
        copy.start()
    obuf[core, :, place] = fin[pl.ds(core * 64, 64)]
    for copy in sends:
        copy.wait_recv()
    out_k[...] = obuf[0]
    out_v[...] = obuf[1]

    def units(v, carry):
        d2d(v).wait_send()
        for c in ys:
            send1(c, v, v // 4, v % 4, 0, 0).wait_send()
            send2(c, v // 4, v % 4, v).wait_send()
        return carry

    lax.fori_loop(0, 16, units, 0)

    def groups(n, carry):
        for c in xs + zs:
            send1(c, 0, 0, 0, 0, n).wait_send()
            send1(c, 0, 0, 0, 1, n).wait_send()
            send2(c, 0, 0, n).wait_send()
        for c in xs:
            x_send3(c, n).wait_send()
        for c in ys:
            y_send3(c, n).wait_send()
        return carry

    lax.fori_loop(0, 4, groups, 0)
    for c in zs:
        z_send3(c, 0).wait_send()
        z_send3(c, 1).wait_send()
        z_send4(c).wait_send()
        z_send5(c).wait_send()
        last(c, "y").wait_send()
    for c in xs:
        x_send4(c).wait_send()
        x_send5(c).wait_send()
        last(c, "z").wait_send()
    for c in ys:
        y_send4(c).wait_send()
        y_send5(c, 0).wait_send()
        y_send5(c, 1).wait_send()
        last(c, "x").wait_send()
    for copy in sends:
        copy.wait_send()


def local(activations, key_cotangent, value_cotangent):
    tok, width = activations.shape
    half = key_cotangent.shape[1]
    rows = width // 64
    dma = pltpu.SemaphoreType.DMA
    return pl.pallas_call(
        kernel,
        out_shape=(jax.ShapeDtypeStruct((rows, half), F32), jax.ShapeDtypeStruct((rows, half), F32)),
        in_specs=[pl.BlockSpec(memory_space=pl.ANY)] * 3,
        out_specs=(pl.BlockSpec(memory_space=pltpu.VMEM), pl.BlockSpec(memory_space=pltpu.VMEM)),
        scratch_shapes=[
            pltpu.VMEM((16, tok, 256), jnp.bfloat16),
            pltpu.VMEM((2, 2, tok, 256), jnp.bfloat16),
            pltpu.VMEM((2, 512, tok), jnp.bfloat16),
            pltpu.VMEM((4, 4, 4, 256, 128), F32),
            pltpu.VMEM((16, 4, 256, 128), F32),
            pltpu.VMEM((16, 4, 256, 128), F32),
            pltpu.VMEM((32, 256, 128), F32),
            pltpu.VMEM((16, 256, 128), F32),
            pltpu.VMEM((8, 256, 128), F32),
            pltpu.VMEM((4, 256, 128), F32),
            pltpu.VMEM((2, 256, 128), F32),
            pltpu.VMEM((256, 128), F32),
            pltpu.VMEM((128, 256), F32),
            pltpu.VMEM((2, rows, half), F32),
            dma((16, 2)), dma((2, 2)), dma((16,)), dma((16,)),
            dma((6, 16)), dma((6, 16)), dma((6, 16)), dma((6, 16)),
            dma((6, 4)), dma((6, 4)), dma((6,)), dma((6,)),
            dma((6, 2)), dma((6, 2)), dma((6,)), dma((6,)),
            dma((3,)), dma((3,)),
        ],
        compiler_params=pltpu.CompilerParams(
            collective_id=0, has_side_effects=True, vmem_limit_bytes=67_043_328
        ),
        name="weight_gradients",
    )(activations, key_cotangent, value_cotangent)


def solution(mesh):
    finer = Mesh(mesh.devices.reshape(mesh.shape["inter"], 4, 2, 4, 2), AXES)
    spec = P(AXES, None)
    out = P(INTRA, None)
    return jax.shard_map(local, mesh=finer, in_specs=(spec, spec, spec), out_specs=(out, out), check_vma=False)
```

time: 292 us -> 94.6 us (0.32)
  the two profiles are of different devices: /device:TPU:0 before, /device:TPU:1 now
where the time goes in v1:
time: 94.6 us; the launch traced here: 94.4 us
  Pallas kernels  90.7 us (96%)
  local copies, waits for them, and re-layouts  3.14 us (3%)
    pallas_call x1, Pallas kernels, local(): pl.pallas_call(kernel, out_shape=(jax.ShapeDtypeStruct((rows, half), F32)...  90.7 us
    unnamed x2, local copies, waits for them, and re-layouts  3.14 us

profile of v1, /device:TPU:1, one launch (start us, length us, event | category | flops | bytes accessed | tf_op | source)
XLA Modules:
  0.0 94.4 jit_solution(13772950439847163863)
XLA Ops:
  0.6 90.7 %weight_gradients.1 = (f32[64,512]{1,0:T(8,128)}, f32[64,512]{1,0:T(8,128)}) custom-call(bf16[2048,4096]{1,0:T(8,128)(2,1)} %a_hbm.1, bf16[2048,512]{1,0:T(8,128)(2,1)} %k_hbm.1, bf16[2048,512]{1,0:T(8,128)(2,1)} %v_hbm.1), custom_call_target="tpu_custom_call" | custom-call | tf_op jit(solution)/shard_map/weight_gradients/pallas_call | solution.py:435
  91.3 1.6 %copy.7 = f32[64,512]{1,0:T(8,128)} copy(f32[64,512]{1,0:T(8,128)} %get-tuple-element.4) | data formatting | bytes 262144
  92.9 1.6 %copy.8 = f32[64,512]{1,0:T(8,128)} copy(f32[64,512]{1,0:T(8,128)} %get-tuple-element.5) | data formatting | bytes 262144

commit v2 on v0

v2 whole, which is shorter than its diff:
```python
import functools

import jax
import jax.numpy as jnp
from jax import lax
from jax.experimental import pallas as pl
from jax.experimental.pallas import tpu as pltpu
from jax.sharding import Mesh
from jax.sharding import PartitionSpec as P

MESH = pl.DeviceIdType.MESH
F32 = jnp.float32
AXES = ("inter", "x", "ylo", "z", "core")
INTRA = ("x", "ylo", "z", "core")

ORDER = {"x": (2, 1, 3, 0), "y": (1, 2, 3, 0), "z": (1, 2, 3, 0)}
SIZES = (48, 40, 40, 40, 48, 40)
KEEP = 3
LAG1 = 1
LAG2 = 3


def flip(r, k):
    if k == 0:
        return r
    if k == 1:
        return r + 1 - 2 * (r % 2)
    if k == 2:
        return (r + 2) % 4
    return 3 - r


def colours():
    result, off = [], 0
    index = 0
    for order in ("xyz", "yzx", "zxy"):
        for p1, p2 in ((1, 3), (3, 1)):
            result.append((index, order, p1, p2, pl.ds(off, SIZES[index])))
            off += SIZES[index]
            index += 1
    return result


def slot(axis, k):
    return ORDER[axis].index(k)


def pair_start(p1):
    return 0 if p1 == 1 else 1


def pair_item(p1, keep):
    first_is_keep = p1 == 1
    return 0 if first_is_keep == keep else 1


def kernel(
    a_hbm, k_hbm, v_hbm, out_k, out_v,
    abuf, cst, ct, acc, dsend, drecv, r1, r2, r3, r4, r5, r6, afar, fin, obuf,
    a_sem, c_sem, ds_sem, dr_sem, s1s, s1r, s2s, s2r, s3s, s3r, s4s, s4r, s5s, s5r, s6s, s6r, fs_sem, fr_sem, es_sem, er_sem,
):
    x, z = lax.axis_index("x"), lax.axis_index("z")
    yhi, ylo = lax.axis_index("inter"), lax.axis_index("ylo")
    core = lax.axis_index("core")
    y = 2 * yhi + ylo
    cols = colours()
    xs, ys, zs = cols[0:2], cols[2:4], cols[4:6]

    def peer(axis, k):
        if axis == "x":
            return {"x": flip(x, k)}
        if axis == "z":
            return {"z": flip(z, k)}
        to = flip(y, k)
        return {"inter": to // 2, "ylo": to % 2}

    other_core = {"core": 1 - core}
    far = {"inter": 1 - yhi}

    barrier = pltpu.get_barrier_semaphore()
    peers = [other_core, far] + [peer(axis, k) for axis in "xyz" for k in (1, 3)]
    for device in peers:
        pl.semaphore_signal(barrier, inc=1, device_id=device, device_id_type=MESH)

    def c_copy(which, hrel):
        src = (k_hbm, v_hbm)[which]
        rel = core if which == 0 else 1 - core
        half = (yhi + hrel) % 2
        return pltpu.make_async_copy(
            src.at[:, pl.ds(pl.multiple_of(half * 256, 256), 256)], cst.at[rel, hrel], c_sem.at[which, hrel]
        )

    def a_start(t):
        for n in range(4):
            tx, tz = flip(x, ORDER["x"][t // 2]), flip(z, ORDER["z"][t % 2 * 2 + n // 2])
            column = pl.multiple_of(((tx * 2 + (ylo + n) % 2) * 4 + tz) * 128, 128)
            pltpu.make_async_copy(
                a_hbm.at[:, pl.ds(column, 128)], abuf.at[t, :, pl.ds(n * 128, 128)], a_sem.at[t]
            ).start()

    with jax.named_scope("cwait"):
        for which in (0, 1):
            for hrel in (0, 1):
                c_copy(which, hrel).start()
        a_start(0)
        for which in (0, 1):
            for hrel in (0, 1):
                c_copy(which, hrel).wait()
    for t in range(1, 8):
        a_start(t)

    def transpose(rel):
        for hrel in (0, 1):
            ct[rel, pl.ds(hrel * 256, 256), :] = cst[rel, hrel].T

    with jax.named_scope("ctrans"):
        transpose(1)

    pl.semaphore_wait(barrier, len(peers))

    def remote(src, dst, send, recv, device):
        return pltpu.make_async_remote_copy(
            src_ref=src, dst_ref=dst, send_sem=send, recv_sem=recv, device_id=device, device_id_type=MESH
        )

    def d2d(t):
        return remote(dsend.at[t], drecv.at[t], ds_sem, dr_sem.at[t], other_core)

    def x_send1(c, sx, sp, i):
        index, _, p1, _, rows = c
        return remote(
            acc.at[sx, pl.ds(2 * sp, 2), :, rows], r1.at[pl.ds(i * 4 + 2 * sp, 2), :, rows],
            s1s, s1r.at[index, i * 2 + sp], peer("x", p1),
        )

    def z_send1(c, sx, sz, i):
        index, _, p1, _, rows = c
        return remote(
            acc.at[sx, sz, :, rows], r1.at[i * 4 + sx, :, rows], s1s, s1r.at[index, i * 4 + sx], peer("z", p1)
        )

    def y_send1(c, t, sx, sp, n):
        index, _, p1, _, rows = c
        return remote(
            acc.at[sx, 2 * sp + n, pl.ds(pair_start(p1), 2), rows], r1.at[t, pl.ds(n * 2, 2), rows],
            s1s, s1r.at[index, t], peer("y", p1),
        )

    def y_wait1(c, t):
        index, _, p1, _, rows = c
        remote(r1.at[t, :, rows], r1.at[t, :, rows], s1s, s1r.at[index, t], peer("y", p1)).wait_recv()

    def x_send2(c, sx, sp):
        index, _, _, p2, rows = c
        return remote(
            acc.at[sx, pl.ds(2 * sp, 2), :, rows], r2.at[pl.ds(2 * sp, 2), :, rows], s2s, s2r.at[index, sp], peer("x", p2)
        )

    def z_send2(c, sx, sz):
        index, _, _, p2, rows = c
        return remote(acc.at[sx, sz, :, rows], r2.at[sx, :, rows], s2s, s2r.at[index, sx], peer("z", p2))

    def y_send2(c, t, sx, sp):
        index, _, _, p2, rows = c
        return remote(
            acc.at[sx, pl.ds(2 * sp, 2), slot("y", p2), rows], r2.at[sx, pl.ds(2 * sp, 2), rows],
            s2s, s2r.at[index, t], peer("y", p2),
        )

    def multiply(t, rel):
        product = jnp.dot(ct[rel], abuf[t], preferred_element_type=F32)
        product = product.astype(jnp.bfloat16).astype(F32)
        for hrel in (0, 1):
            for n in range(4):
                yield n // 2, slot("y", 2 * hrel + n % 2), product[hrel * 256 : hrel * 256 + 256, n * 128 : n * 128 + 128]

    def for_other(t):
        pltpu.make_async_copy(abuf.at[t], abuf.at[t], a_sem.at[t]).wait()
        for n, target, block in multiply(t, 1):
            dsend[t, n, target] = block
        d2d(t).start()

    def own(t):
        sx, sp = t // 2, t % 2
        with jax.named_scope("d2dwait"):
            d2d(t).wait_recv()
        with jax.named_scope("dotown"):
            for n, target, block in multiply(t, 0):
                acc[sx, 2 * sp + n, target] = block + drecv[t, n, target]
        for c in xs:
            for i, k in ((0, 2), (1, c[2])):

                @pl.when(sx == slot("x", k))
                def _(c=c, i=i):
                    x_send1(c, sx, sp, i).start()

        for c in zs:
            for i, k in ((0, 2), (1, c[2])):
                sz = slot("z", k)

                @pl.when(sp == sz // 2)
                def _(c=c, i=i, sz=sz):
                    z_send1(c, sx, sz, i).start()

        for c in ys:
            for n in (0, 1):
                y_send1(c, t, sx, sp, n).start()

    def second(t):
        sx, sp = t // 2, t % 2
        for c in xs:
            p2, rows = c[3], c[4]

            @pl.when(sx == slot("x", p2))
            def _(c=c, rows=rows):
                x_send1(c, sx, sp, 0).wait_recv()
                acc[sx, pl.ds(2 * sp, 2), :, rows] = acc[sx, pl.ds(2 * sp, 2), :, rows] + r1[pl.ds(2 * sp, 2), :, rows]
                x_send2(c, sx, sp).start()

        for c in zs:
            p2, rows = c[3], c[4]

            @pl.when(sp == 1)
            def _(c=c, p2=p2, rows=rows):
                on = slot("z", p2)
                z_send1(c, sx, on, 0).wait_recv()
                acc[sx, on, :, rows] = acc[sx, on, :, rows] + r1[sx, :, rows]
                z_send2(c, sx, on).start()

        for c in ys:
            _, _, p1, p2, rows = c
            on = slot("y", p2)
            y_wait1(c, t)
            for n in (0, 1):
                sz = 2 * sp + n
                acc[sx, sz, on, rows] = acc[sx, sz, on, rows] + r1[t, n * 2 + pair_item(p1, False), rows]
                acc[sx, sz, KEEP, rows] = acc[sx, sz, KEEP, rows] + r1[t, n * 2 + pair_item(p1, True), rows]
            y_send2(c, t, sx, sp).start()

    def step(u, carry):
        @pl.when(u < 8)
        def _():
            with jax.named_scope("dotsend"):
                for_other(u)

        @pl.when(u == 0)
        def _():
            transpose(0)

        @pl.when((u >= LAG1) & (u < 8 + LAG1))
        def _():
            own(u - LAG1)

        @pl.when(u >= LAG2)
        def _():
            with jax.named_scope("second"):
                second(u - LAG2)

        return carry

    lax.fori_loop(0, 8 + LAG2, step, 0)

    def x_send3(c, sz):
        index, _, p1, _, rows = c
        return remote(
            acc.at[3, sz, pl.ds(pair_start(p1), 2), rows], r3.at[pl.ds(sz * 2, 2), rows], s3s, s3r.at[index, sz], peer("y", p1)
        )

    def y_send3(c, sx):
        index, _, p1, _, rows = c
        return remote(
            acc.at[sx, pl.ds(pair_start(p1), 2), KEEP, rows], r3.at[pl.ds(sx * 2, 2), rows],
            s3s, s3r.at[index, sx], peer("z", p1),
        )

    def z_send3(c, i):
        index, _, p1, _, rows = c
        sx = slot("x", (2, p1)[i])
        return remote(acc.at[sx, KEEP, :, rows], r3.at[pl.ds(i * 4, 4), rows], s3s, s3r.at[index, i], peer("x", p1))

    with jax.named_scope("x3"):
        for sp in (0, 1):
            for c in xs:
                rows = c[4]
                x_send1(c, 0, sp, 1).wait_recv()
                x_send2(c, 0, sp).wait_recv()
                for sz in (2 * sp, 2 * sp + 1):
                    acc[3, sz, :, rows] = acc[3, sz, :, rows] + (r1[4 + sz, :, rows] + r2[sz, :, rows])
                    x_send3(c, sz).start()

    with jax.named_scope("zy3"):
        for sx in range(4):
            for c in zs:
                _, _, p1, _, rows = c
                z_send1(c, sx, 0, 1).wait_recv()
                z_send2(c, sx, 0).wait_recv()
                acc[sx, 3, :, rows] = acc[sx, 3, :, rows] + (r1[4 + sx, :, rows] + r2[sx, :, rows])
                for i in (0, 1):
                    if sx == slot("x", (2, p1)[i]):
                        z_send3(c, i).start()
            for c in ys:
                rows = c[4]
                for sp in (0, 1):
                    y_send2(c, sx * 2 + sp, sx, sp).wait_recv()
                acc[sx, :, KEEP, rows] = acc[sx, :, KEEP, rows] + r2[sx, :, rows]
                y_send3(c, sx).start()

    def x_send4(c):
        index, _, _, p2, rows = c
        return remote(acc.at[3, :, slot("y", p2), rows], r4.at[:, rows], s4s, s4r.at[index], peer("y", p2))

    def y_send4(c):
        index, _, _, p2, rows = c
        return remote(acc.at[:, slot("z", p2), KEEP, rows], r4.at[:, rows], s4s, s4r.at[index], peer("z", p2))

    def z_send4(c):
        index, _, _, p2, rows = c
        return remote(acc.at[slot("x", p2), KEEP, :, rows], r4.at[:, rows], s4s, s4r.at[index], peer("x", p2))

    with jax.named_scope("x4"):
        for c in xs:
            _, _, p1, p2, rows = c
            on = slot("y", p2)
            for sz in range(4):
                x_send3(c, sz).wait_recv()
                acc[3, sz, on, rows] = acc[3, sz, on, rows] + r3[sz * 2 + pair_item(p1, False), rows]
                acc[3, sz, KEEP, rows] = acc[3, sz, KEEP, rows] + r3[sz * 2 + pair_item(p1, True), rows]
            x_send4(c).start()
    with jax.named_scope("z4"):
        for c in zs:
            _, _, p1, p2, rows = c
            on = slot("x", p2)
            z_send3(c, 0).wait_recv()
            acc[on, KEEP, :, rows] = acc[on, KEEP, :, rows] + r3[pl.ds(0, 4), rows]
            z_send4(c).start()
    with jax.named_scope("y4"):
        for c in ys:
            _, _, p1, p2, rows = c
            on = slot("z", p2)
            for sx in range(4):
                y_send3(c, sx).wait_recv()
                acc[sx, on, KEEP, rows] = acc[sx, on, KEEP, rows] + r3[sx * 2 + pair_item(p1, False), rows]
                acc[sx, 3, KEEP, rows] = acc[sx, 3, KEEP, rows] + r3[sx * 2 + pair_item(p1, True), rows]
            y_send4(c).start()

    def x_send5(c):
        index, _, p1, _, rows = c
        return remote(
            acc.at[3, pl.ds(pair_start(p1), 2), KEEP, rows], r5.at[:, rows], s5s, s5r.at[index, 0], peer("z", p1)
        )

    def z_send5(c):
        index, _, p1, _, rows = c
        return remote(
            acc.at[3, KEEP, pl.ds(pair_start(p1), 2), rows], r5.at[:, rows], s5s, s5r.at[index, 0], peer("y", p1)
        )

    def y_send5(c, i):
        index, _, p1, _, rows = c
        return remote(
            acc.at[slot("x", (2, p1)[i]), KEEP, KEEP, rows], r5.at[i, rows], s5s, s5r.at[index, i], peer("x", p1)
        )

    with jax.named_scope("x5"):
        for c in xs:
            rows = c[4]
            x_send4(c).wait_recv()
            acc[3, :, KEEP, rows] = acc[3, :, KEEP, rows] + r4[:, rows]
            x_send5(c).start()
    with jax.named_scope("z5"):
        for c in zs:
            _, _, p1, _, rows = c
            z_send3(c, 1).wait_recv()
            z_send4(c).wait_recv()
            acc[3, KEEP, :, rows] = acc[3, KEEP, :, rows] + (r3[pl.ds(4, 4), rows] + r4[:, rows])
            z_send5(c).start()
    with jax.named_scope("y5"):
        for c in ys:
            rows = c[4]
            y_send4(c).wait_recv()
            acc[:, 3, KEEP, rows] = acc[:, 3, KEEP, rows] + r4[:, rows]
            for i in (0, 1):
                y_send5(c, i).start()

    def last(c, axis):
        index, _, _, p2, rows = c
        on = slot(axis, p2)
        src = {"x": acc.at[on, KEEP, KEEP, rows], "y": acc.at[3, KEEP, on, rows], "z": acc.at[3, on, KEEP, rows]}[axis]
        return remote(src, r6.at[rows], s6s, s6r.at[index], peer(axis, p2))

    def to_far(c):
        index, rows = c[0], c[4]
        return remote(acc.at[3, KEEP, KEEP, rows], afar.at[rows], fs_sem, fr_sem.at[index], far)

    groups = ((xs, "z"), (zs, "y"), (ys, "x"))
    for group, axis in groups:
        with jax.named_scope("last" + axis):
            for c in group:
                _, _, p1, p2, rows = c
                on = slot(axis, p2)
                if axis == "x":
                    y_send5(c, 0).wait_recv()
                    y_send5(c, 1).wait_recv()
                    onward, kept = r5[0, rows], r5[1, rows]
                    acc[on, KEEP, KEEP, rows] = acc[on, KEEP, KEEP, rows] + onward
                else:
                    (x_send5 if axis == "z" else z_send5)(c).wait_recv()
                    onward, kept = r5[pair_item(p1, False), rows], r5[pair_item(p1, True), rows]
                    if axis == "z":
                        acc[3, on, KEEP, rows] = acc[3, on, KEEP, rows] + onward
                    else:
                        acc[3, KEEP, on, rows] = acc[3, KEEP, on, rows] + onward
                last(c, axis).start()
                acc[3, KEEP, KEEP, rows] = acc[3, KEEP, KEEP, rows] + kept

    for group, axis in groups:
        with jax.named_scope("far" + axis):
            for c in group:
                rows = c[4]
                last(c, axis).wait_recv()
                acc[3, KEEP, KEEP, rows] = acc[3, KEEP, KEEP, rows] + r6[rows]
                to_far(c).start()

    own_place = pl.ds(pl.multiple_of(yhi * 256, 256), 256)
    far_place = pl.ds(pl.multiple_of((1 - yhi) * 256, 256), 256)

    def swap(n, place):
        return remote(
            fin.at[n, pl.ds((1 - core) * 64, 64)], obuf.at[core, :, place], es_sem.at[n], er_sem.at[n], other_core
        )

    with jax.named_scope("swap0"):
        fin[0] = acc[3, KEEP, KEEP].T
        swap(0, own_place).start()
        obuf[core, :, own_place] = fin[0, pl.ds(core * 64, 64)]
    with jax.named_scope("farwait"):
        for c in cols:
            to_far(c).wait_recv()
    with jax.named_scope("swap1"):
        fin[1] = afar[...].T
        swap(1, far_place).start()
        obuf[core, :, far_place] = fin[1, pl.ds(core * 64, 64)]
        swap(0, own_place).wait_recv()
        swap(1, far_place).wait_recv()
        out_k[...] = obuf[0]
        out_v[...] = obuf[1]

    with jax.named_scope("ends"):
        for whole, sem in (
            (drecv, ds_sem), (r1, s1s), (r2, s2s), (r3, s3s), (r4, s4s), (r5, s5s), (r6, s6s), (afar, fs_sem)
        ):
            remote(whole, whole, sem, er_sem.at[0], other_core).wait_send()
        for n, place in ((0, own_place), (1, far_place)):
            swap(n, place).wait_send()


def local(activations, key_cotangent, value_cotangent):
    tok, width = activations.shape
    half = key_cotangent.shape[1]
    rows = width // 64
    dma = pltpu.SemaphoreType.DMA
    return pl.pallas_call(
        kernel,
        out_shape=(jax.ShapeDtypeStruct((rows, half), F32), jax.ShapeDtypeStruct((rows, half), F32)),
        in_specs=[pl.BlockSpec(memory_space=pl.ANY)] * 3,
        out_specs=(pl.BlockSpec(memory_space=pltpu.VMEM), pl.BlockSpec(memory_space=pltpu.VMEM)),
        scratch_shapes=[
            pltpu.VMEM((8, tok, 512), jnp.bfloat16),
            pltpu.VMEM((2, 2, tok, 256), jnp.bfloat16),
            pltpu.VMEM((2, 512, tok), jnp.bfloat16),
            pltpu.VMEM((4, 4, 4, 256, 128), F32),
            pltpu.VMEM((8, 2, 4, 256, 128), F32),
            pltpu.VMEM((8, 2, 4, 256, 128), F32),
            pltpu.VMEM((8, 4, 256, 128), F32),
            pltpu.VMEM((4, 4, 256, 128), F32),
            pltpu.VMEM((8, 256, 128), F32),
            pltpu.VMEM((4, 256, 128), F32),
            pltpu.VMEM((2, 256, 128), F32),
            pltpu.VMEM((256, 128), F32),
            pltpu.VMEM((256, 128), F32),
            pltpu.VMEM((2, 128, 256), F32),
            pltpu.VMEM((2, rows, half), F32),
            dma((8,)), dma((2, 2)), dma, dma((8,)),
            dma, dma((6, 8)), dma, dma((6, 8)),
            dma, dma((6, 4)), dma, dma((6,)),
            dma, dma((6, 2)), dma, dma((6,)),
            dma, dma((6,)), dma((2,)), dma((2,)),
        ],
        compiler_params=pltpu.CompilerParams(
            collective_id=0, has_side_effects=True, vmem_limit_bytes=67_043_328
        ),
        name="weight_gradients",
    )(activations, key_cotangent, value_cotangent)


def solution(mesh):
    finer = Mesh(mesh.devices.reshape(mesh.shape["inter"], 4, 2, 4, 2), AXES)
    spec = P(AXES, None)
    out = P(INTRA, None)
    return jax.shard_map(local, mesh=finer, in_specs=(spec, spec, spec), out_specs=(out, out), check_vma=False)
```

time: 292 us -> 69.5 us (0.24)
  the two profiles are of different devices: /device:TPU:0 before, /device:TPU:1 now
where the time goes in v2:
time: 69.5 us; the launch traced here: 69.3 us
  Pallas kernels  65.6 us (94%)
  local copies, waits for them, and re-layouts  3.14 us (5%)
    pallas_call x1, Pallas kernels, local(): pl.pallas_call(kernel, out_shape=(jax.ShapeDtypeStruct((rows, half), F32)...  65.6 us
    unnamed x2, local copies, waits for them, and re-layouts  3.14 us

profile of v2, /device:TPU:1, one launch (start us, length us, event | category | flops | bytes accessed | tf_op | source)
XLA Modules:
  0.0 69.3 jit_solution(15641027584245487303)
XLA Ops:
  0.6 65.6 %weight_gradients.1 = (f32[64,512]{1,0:T(8,128)}, f32[64,512]{1,0:T(8,128)}) custom-call(bf16[2048,4096]{1,0:T(8,128)(2,1)} %a_hbm.1, bf16[2048,512]{1,0:T(8,128)(2,1)} %k_hbm.1, bf16[2048,512]{1,0:T(8,128)(2,1)} %v_hbm.1), custom_call_target="tpu_custom_call" | custom-call | tf_op jit(solution)/shard_map/weight_gradients/pallas_call | solution.py:462
  66.2 1.6 %copy.7 = f32[64,512]{1,0:T(8,128)} copy(f32[64,512]{1,0:T(8,128)} %get-tuple-element.4) | data formatting | bytes 262144
  67.8 1.6 %copy.8 = f32[64,512]{1,0:T(8,128)} copy(f32[64,512]{1,0:T(8,128)} %get-tuple-element.5) | data formatting | bytes 262144

commit v3 on v0

v3 whole, which is shorter than its diff:
```python
import jax
import jax.numpy as jnp
from jax import lax
from jax.experimental import pallas as pl
from jax.experimental.pallas import tpu as pltpu
from jax.sharding import Mesh
from jax.sharding import PartitionSpec as P

MESH = pl.DeviceIdType.MESH
F32 = jnp.float32
AXES = ("inter", "x", "ylo", "z", "core")
INTRA = ("x", "ylo", "z", "core")

UNIT_ORDER = (2, 0, 1, 3)
ORDER = (1, 2, 3, 0)
KEEP = 3
SIZES = ((24, 16, 24, 24, 16, 24), (16, 24, 24, 16, 24, 24))
LAG1 = 2
LAG2 = 5


def flip(r, k):
    if k == 0:
        return r
    if k == 1:
        return r + 1 - 2 * (r % 2)
    if k == 2:
        return (r + 2) % 4
    return 3 - r


def colours(wave):
    result, off = [], 0
    for order in ("yzx", "xyz", "zxy"):
        for p1, p2 in ((1, 3), (3, 1)):
            size = SIZES[wave][len(result)]
            result.append((len(result), order, p1, p2, pl.ds(off, size)))
            off += size
    return result


def pair_start(p1):
    return 0 if p1 == 1 else 1


def onward_item(p1):
    return 1 if p1 == 1 else 0


def kept_item(p1):
    return 1 - onward_item(p1)


def unit_at(sx, sz):
    return (sx // 2) * 4 + (sz // 2) * 2 + (sx + sz) % 2, sx % 2


def kernel(
    a_hbm, k_hbm, v_hbm, out,
    abuf, cst, ct, acc, dsend, drecv, r1, r1y, r2, b2, r3, r4, fin, obuf,
    a_sem, c_sem, ds_sem, dr_sem, s1s, s1r, s2s, s2r, s3s, s3r, s4s, s4r, es_sem, er_sem,
):
    x, z = lax.axis_index("x"), lax.axis_index("z")
    yhi, ylo = lax.axis_index("inter"), lax.axis_index("ylo")
    core = lax.axis_index("core")
    y = 2 * yhi + ylo

    def peer(axis, k):
        if axis == "x":
            return {"x": flip(x, k)}
        if axis == "z":
            return {"z": flip(z, k)}
        to = flip(y, k)
        return {"inter": to // 2, "ylo": to % 2}

    other_core = {"core": 1 - core}
    far = {"inter": 1 - yhi}
    far_other = {"inter": 1 - yhi, "core": 1 - core}

    barrier = pltpu.get_barrier_semaphore()
    peers = [other_core, far_other] + [peer(axis, k) for axis in "xyz" for k in (1, 2, 3)]
    for device in peers:
        pl.semaphore_signal(barrier, inc=1, device_id=device, device_id_type=MESH)

    def c_start(wave, priority):
        for which, src in ((0, k_hbm), (1, v_hbm)):
            rel = core if which == 0 else 1 - core
            for hrel in (0, 1):
                half = (yhi + hrel) % 2
                pltpu.make_async_copy(
                    src.at[:, pl.ds(pl.multiple_of(half * 256 + wave * 128, 128), 128)], cst.at[wave, rel, hrel], c_sem.at[wave]
                ).start(priority=priority)

    def c_wait(wave):
        pltpu.make_async_copy(cst.at[wave], cst.at[wave], c_sem.at[wave]).wait()

    def a_start(t, priority):
        for n in (0, 1):
            tx, tz = flip(x, UNIT_ORDER[t // 4 * 2 + n]), flip(z, UNIT_ORDER[t // 2 % 2 * 2 + (n + t) % 2])
            for lrel in (0, 1):
                column = pl.multiple_of(((tx * 2 + (ylo + lrel) % 2) * 4 + tz) * 128, 128)
                pltpu.make_async_copy(
                    a_hbm.at[:, pl.ds(column, 128)], abuf.at[t, :, pl.ds((n * 2 + lrel) * 128, 128)], a_sem.at[t]
                ).start(priority=priority)

    with jax.named_scope("cwait"):
        c_start(0, 0)
        a_start(0, 0)
        a_start(1, 1)
        c_start(1, 1)
        for t in range(2, 8):
            a_start(t, 1)
        c_wait(0)

    def transpose(rel, wave):
        for hrel in (0, 1):
            ct[rel, wave, pl.ds(hrel * 128, 128), :] = cst[wave, rel, hrel].T

    with jax.named_scope("ctrans"):
        transpose(1, 0)

    def remote(src, dst, send, recv, device):
        return pltpu.make_async_remote_copy(
            src_ref=src, dst_ref=dst, send_sem=send, recv_sem=recv, device_id=device, device_id_type=MESH
        )

    def d2d(g):
        return remote(dsend.at[g], drecv.at[g], ds_sem, dr_sem.at[g % 4], other_core)

    def first_sem(c, w, which):
        index = c[0]
        return s1r.at[w, index * 8 + which] if index < 2 else s1r.at[w, 16 + (index - 2) * 3 + which]

    def send1(c, w, t):
        index, order, p1, _, rows = c
        xt, zt, m = t // 4, t // 2 % 2, t % 2
        device = peer(order[0], p1)
        if order[0] == "y":
            return remote(
                acc.at[w, t, :, pl.ds(pair_start(p1), 2), rows], r1y.at[w, t, :, :, rows], s1s, first_sem(c, w, t), device
            )
        if order[0] == "x":
            n = 0 if p1 == 1 else xt
            item = xt * 4 + zt * 2 + (n + m) % 2
            sem = first_sem(c, w, 2 * xt)
        else:
            n = m if p1 == 1 else (m + zt) % 2
            item = zt * 4 + xt * 2 + n
            sem = first_sem(c, w, xt + zt * (2 - xt))
        return remote(acc.at[w, t, n, :, rows], r1.at[w, item, :, rows], s1s, sem, device)

    def wait_for(ref, sem):
        remote(ref, ref, s1s, sem, other_core).wait_recv()

    def send2(c, w, t, n, item):
        index, order, _, p2, rows = c
        device = peer(order[0], p2)
        if order[0] == "y":
            return remote(
                acc.at[w, t, :, ORDER.index(p2), rows], r2.at[w, t // 2, pl.ds(t % 2 * 2, 2), rows], s2s, s2r.at[w, index], device
            )
        return remote(acc.at[w, t, n, :, rows], r2.at[w, item, :, rows], s2s, s2r.at[w, index], device)

    def multiply(t, w, rel):
        product = jnp.dot(ct[rel, w], abuf[t], preferred_element_type=F32)
        product = product.astype(jnp.bfloat16).astype(F32)
        for hrel in (0, 1):
            for n in (0, 1):
                for lrel in (0, 1):
                    place = (n * 2 + lrel) * 128
                    yield n, ORDER.index(2 * hrel + lrel), product[hrel * 128 : hrel * 128 + 128, place : place + 128]

    def a_wait(g):
        pltpu.make_async_copy(abuf.at[g], abuf.at[g], a_sem.at[g]).wait()

    def for_other(g):
        for n, target, block in multiply(g % 8, g // 8, 1):
            dsend[g, n, target] = block

    def own(g):
        for n, target, block in multiply(g % 8, g // 8, 0):
            acc[g // 8, g % 8, n, target] = block + drecv[g, n, target]

    def first(g):
        for wave in (0, 1):

            @pl.when(g // 8 == wave)
            def _(wave=wave):
                for c in colours(wave):
                    send1(c, wave, g % 8).start()

    def second(w, t):
        xt, zt, m = t // 4, t // 2 % 2, t % 2

        def onward(c, n, item):
            rows = c[4]
            acc[w, t, n, :, rows] = acc[w, t, n, :, rows] + r1[w, item, :, rows]
            send2(c, w, t, n, item).start()

        ys, xs, zs = colours(w)[0:2], colours(w)[2:4], colours(w)[4:6]
        for c in ys:
            _, _, p1, p2, rows = c
            on = ORDER.index(p2)
            send1(c, w, t).wait_recv()
            for n in (0, 1):
                acc[w, t, n, on, rows] = acc[w, t, n, on, rows] + r1y[w, t, n, onward_item(p1), rows]
            send2(c, w, t, 0, 0).start()

        @pl.when(t == 4)
        def _():
            for c in xs:
                wait_for(r1.at[w, pl.ds(0, 4), :, c[4]], first_sem(c, w, 0))

        @pl.when((zt == 1) & (m == 0))
        def _():
            for c in zs:
                wait_for(r1.at[w, pl.ds(0, 2), :, c[4]], first_sem(c, w, xt))

        @pl.when(xt == 1)
        def _():
            for c in xs:
                n = 1 if c[2] == 1 else 0
                onward(c, n, zt * 2 + (n + m) % 2)

        @pl.when(zt == 1)
        def _():
            for c in zs:
                n = 1 - m if c[2] == 1 else m
                onward(c, n, xt * 2 + n)

    def stage1(w):
        for c in colours(w)[2:6]:
            index, order, p1, _, rows = c
            wait_for(r1.at[w, pl.ds(4, 4), :, rows], first_sem(c, w, 2))
            wait_for(r2.at[w, :, :, rows], s2r.at[w, index])
            for item in range(4):
                t, n = unit_at(1, item) if order[0] == "x" else unit_at(item, 1)
                total = acc[w, t, n, :, rows] + (r1[w, 4 + item, :, rows] + r2[w, item, :, rows])
                place = ORDER.index(UNIT_ORDER[item])
                if order[0] == "x":
                    b2[w, :, place, rows] = total
                else:
                    b2[w, place, :, rows] = total
            spread2(c, w)
        for c in colours(w)[0:2]:
            index, _, p1, _, rows = c
            wait_for(r2.at[w, :, :, rows], s2r.at[w, index])
            for sx in range(4):
                for sz in range(4):
                    t, n = unit_at(sx, sz)
                    total = acc[w, t, n, KEEP, rows] + (r1y[w, t, n, kept_item(p1), rows] + r2[w, t // 2, t % 2 * 2 + n, rows])
                    b2[w, ORDER.index(UNIT_ORDER[sz]), ORDER.index(UNIT_ORDER[sx]), rows] = total
            spread2(c, w)

    def spread2(c, w):
        index, order, _, _, rows = c
        for n, k in enumerate(ORDER[:3]):
            remote(b2.at[w, n, :, rows], r3.at[w, n, :, rows], s3s, s3r.at[w, index], peer(order[1], k)).start()

    def spread3(c, w):
        index, order, _, _, rows = c
        for n, k in enumerate(ORDER[:3]):
            remote(b2.at[w, KEEP, n, rows], r4.at[w, n, rows], s4s, s4r.at[w, index], peer(order[2], k)).start()

    def in_order(w):
        every = colours(w)
        return every[2:6] + every[0:2]

    def stage2(w):
        for c in in_order(w):
            index, rows = c[0], c[4]
            wait_for(r3.at[w, :, :, rows], s3r.at[w, index])
            b2[w, KEEP, :, rows] = (b2[w, KEEP, :, rows] + r3[w, 0, :, rows]) + (r3[w, 1, :, rows] + r3[w, 2, :, rows])
            spread3(c, w)

    def stage3(w):
        for c in in_order(w):
            index, rows = c[0], c[4]
            wait_for(r4.at[w, :, rows], s4r.at[w, index])
            b2[w, KEEP, KEEP, rows] = (b2[w, KEEP, KEEP, rows] + r4[w, 0, rows]) + (r4[w, 1, rows] + r4[w, 2, rows])

    def spread4(w, n):
        to_core, device = ((core, far), (1 - core, far_other), (1 - core, other_core))[n]
        return remote(
            fin.at[w, pl.ds(to_core * 64, 64)],
            obuf.at[core, :, pl.ds(pl.multiple_of(yhi * 256 + w * 128, 128), 128)],
            es_sem, er_sem.at[w, n], device,
        )

    def stage4(w):
        fin[w] = b2[w, KEEP, KEEP].T
        for n in range(3):
            spread4(w, n).start()
        obuf[core, :, pl.ds(pl.multiple_of(yhi * 256 + w * 128, 128), 128)] = fin[w, pl.ds(core * 64, 64)]

    with jax.named_scope("start"):
        a_wait(0)
        for_other(0)
        pl.semaphore_wait(barrier, len(peers))
        d2d(0).start()
        transpose(0, 0)
        a_wait(1)
        for_other(1)
        d2d(1).start()

    def step(g, carry):
        @pl.when(g < 8)
        def _():
            a_wait(g)

        with jax.named_scope("d2dwait"):
            d2d(g - LAG1).wait_recv()
        with jax.named_scope("dots"):
            for_other(g)
            own(g - LAG1)
        d2d(g).start()
        first(g - LAG1)

        @pl.when(g == 3)
        def _():
            c_wait(1)
            transpose(1, 1)
            transpose(0, 1)

        for wave in (0, 1):

            @pl.when((g >= LAG2 + 8 * wave) & (g < LAG2 + 8 * wave + 8))
            def _(wave=wave):
                with jax.named_scope("second"):
                    second(wave, g - LAG2 - 8 * wave)

        return carry

    lax.fori_loop(LAG1, 16, step, 0)

    for g in range(16, 16 + LAG2):
        if g < 16 + LAG1:
            with jax.named_scope("own"):
                d2d(g - LAG1).wait_recv()
                own(g - LAG1)
                for c in colours(1):
                    send1(c, 1, g - LAG1 - 8).start()
        with jax.named_scope("second"):
            second(1, g - LAG2 - 8)
        if g == 17:
            with jax.named_scope("e1"):
                stage1(0)

    for name, stage, w in (
        ("f1", stage1, 1), ("e2", stage2, 0), ("f2", stage2, 1), ("e3", stage3, 0), ("e4", stage4, 0),
        ("f3", stage3, 1), ("f4", stage4, 1),
    ):
        with jax.named_scope(name):
            stage(w)

    with jax.named_scope("swapwait"):
        for w in (0, 1):
            for n in range(3):
                spread4(w, n).wait_recv()
        out[...] = obuf[...]

    with jax.named_scope("ends"):
        for wave in (0, 1):
            rest = colours(wave)[2:6]
            for whole in (
                r1y.at[wave, :, :, :, pl.ds(0, SIZES[wave][0] + SIZES[wave][1])],
                r1.at[wave, :, :, pl.ds(rest[0][4].start, 128 - rest[0][4].start)],
            ):
                remote(whole, whole, s1s, er_sem.at[0, 0], other_core).wait_send()
        for whole, sem in (
            (drecv, ds_sem), (r2, s2s), (r3, s3s), (r4, s4s), (drecv.at[0, 0, pl.ds(0, 3)], es_sem)
        ):
            remote(whole, whole, sem, er_sem.at[0, 0], other_core).wait_send()


def local(activations, key_cotangent, value_cotangent):
    tok, width = activations.shape
    half = key_cotangent.shape[1]
    rows = width // 64
    y_rows = max(sizes[0] + sizes[1] for sizes in SIZES)
    dma = pltpu.SemaphoreType.DMA
    both = pl.pallas_call(
        kernel,
        out_shape=jax.ShapeDtypeStruct((2, rows, half), F32),
        in_specs=[pl.BlockSpec(memory_space=pl.ANY)] * 3,
        out_specs=pl.BlockSpec(memory_space=pltpu.VMEM),
        scratch_shapes=[
            pltpu.VMEM((8, tok, 512), jnp.bfloat16),
            pltpu.VMEM((2, 2, 2, tok, 128), jnp.bfloat16),
            pltpu.VMEM((2, 2, 256, tok), jnp.bfloat16),
            pltpu.VMEM((2, 8, 2, 4, 128, 128), F32),
            pltpu.VMEM((16, 2, 4, 128, 128), F32),
            pltpu.VMEM((16, 2, 4, 128, 128), F32),
            pltpu.VMEM((2, 8, 4, 128, 128), F32),
            pltpu.VMEM((2, 8, 2, 2, y_rows, 128), F32),
            pltpu.VMEM((2, 4, 4, 128, 128), F32),
            pltpu.VMEM((2, 4, 4, 128, 128), F32),
            pltpu.VMEM((2, 3, 4, 128, 128), F32),
            pltpu.VMEM((2, 3, 128, 128), F32),
            pltpu.VMEM((2, 128, 128), F32),
            pltpu.VMEM((2, rows, half), F32),
            dma((8,)), dma((2,)), dma, dma((4,)),
            dma, dma((2, 28)), dma, dma((2, 6)),
            dma, dma((2, 6)), dma, dma((2, 6)),
            dma, dma((2, 3)),
        ],
        compiler_params=pltpu.CompilerParams(
            collective_id=0, has_side_effects=True, vmem_limit_bytes=67_043_328
        ),
        name="weight_gradients",
    )(activations, key_cotangent, value_cotangent)
    return both[0], both[1]


def solution(mesh):
    finer = Mesh(mesh.devices.reshape(mesh.shape["inter"], 4, 2, 4, 2), AXES)
    spec = P(AXES, None)
    out = P(INTRA, None)
    return jax.shard_map(local, mesh=finer, in_specs=(spec, spec, spec), out_specs=(out, out), check_vma=False)
```

time: 292 us -> 64.2 us (0.22)
  the two profiles are of different devices: /device:TPU:0 before, /device:TPU:1 now
where the time goes in v3:
time: 64.2 us; the launch traced here: 64.1 us
  Pallas kernels  61.8 us (96%)
  local copies, waits for them, and re-layouts  1.69 us (3%)
    pallas_call x1, Pallas kernels, local(): pl.pallas_call(kernel, out_shape=jax.ShapeDtypeStruct((2, rows, half), F3...  61.8 us
    squeeze x1, local copies, waits for them, and re-layouts, local(): return (both[0], both[1])  1.69 us

profile of v3, /device:TPU:1, one launch (start us, length us, event | category | flops | bytes accessed | tf_op | source)
XLA Modules:
  0.0 64.1 jit_solution(12325674139410857128)
XLA Ops:
  0.6 61.8 %weight_gradients.1 = f32[2,64,512]{2,1,0:T(8,128)} custom-call(bf16[2048,4096]{1,0:T(8,128)(2,1)} %a_hbm.1, bf16[2048,512]{1,0:T(8,128)(2,1)} %k_hbm.1, bf16[2048,512]{1,0:T(8,128)(2,1)} %v_hbm.1), custom_call_target="tpu_custom_call" | custom-call | tf_op jit(solution)/shard_map/weight_gradients/pallas_call | solution.py:382
  62.4 1.7 %slice_bitcast_fusion = (f32[64,512]{1,0:T(8,128)}, f32[64,512]{1,0:T(8,128)}) fusion(f32[2,64,512]{2,1,0:T(8,128)} %weight_gradients.1), kind=kLoop, calls=%fused_computation | loop fusion | bytes 524288 | tf_op jit(solution)/shard_map/squeeze | solution.py:412

commit v4 on v3

--- a/solution.py
+++ b/solution.py
@@ -14,6 +14,8 @@
 UNIT_ORDER = (2, 0, 1, 3)
 ORDER = (1, 2, 3, 0)
 KEEP = 3
+LIMIT = 52 * 1024 * 1024
+FAR_FIRST = (1, 0, 2)
 SIZES = ((24, 16, 24, 24, 16, 24), (16, 24, 24, 16, 24, 24))
 LAG1 = 2
 LAG2 = 5
@@ -125,7 +127,7 @@
         )
 
     def d2d(g):
-        return remote(dsend.at[g], drecv.at[g], ds_sem, dr_sem.at[g % 4], other_core)
+        return remote(dsend.at[g % 4], drecv.at[g % 4], ds_sem.at[g % 4], dr_sem.at[g % 4], other_core)
 
     def first_sem(c, w, which):
         index = c[0]
@@ -175,11 +177,11 @@
 
     def for_other(g):
         for n, target, block in multiply(g % 8, g // 8, 1):
-            dsend[g, n, target] = block
+            dsend[g % 4, n, target] = block
 
     def own(g):
         for n, target, block in multiply(g % 8, g // 8, 0):
-            acc[g // 8, g % 8, n, target] = block + drecv[g, n, target]
+            acc[g // 8, g % 8, n, target] = block + drecv[g % 4, n, target]
 
     def first(g):
         for wave in (0, 1):
@@ -254,12 +256,14 @@
 
     def spread2(c, w):
         index, order, _, _, rows = c
-        for n, k in enumerate(ORDER[:3]):
+        for n in FAR_FIRST:
+            k = ORDER[n]
             remote(b2.at[w, n, :, rows], r3.at[w, n, :, rows], s3s, s3r.at[w, index], peer(order[1], k)).start()
 
     def spread3(c, w):
         index, order, _, _, rows = c
-        for n, k in enumerate(ORDER[:3]):
+        for n in FAR_FIRST:
+            k = ORDER[n]
             remote(b2.at[w, KEEP, n, rows], r4.at[w, n, rows], s4s, s4r.at[w, index], peer(order[2], k)).start()
 
     def in_order(w):
@@ -296,9 +300,9 @@
     with jax.named_scope("start"):
         a_wait(0)
         for_other(0)
+        transpose(0, 0)
         pl.semaphore_wait(barrier, len(peers))
         d2d(0).start()
-        transpose(0, 0)
         a_wait(1)
         for_other(1)
         d2d(1).start()
@@ -307,6 +311,10 @@
         @pl.when(g < 8)
         def _():
             a_wait(g)
+
+        @pl.when(g >= 4)
+        def _():
+            d2d(g).wait_send()
 
         with jax.named_scope("d2dwait"):
             d2d(g - LAG1).wait_recv()
@@ -342,12 +350,8 @@
                     send1(c, 1, g - LAG1 - 8).start()
         with jax.named_scope("second"):
             second(1, g - LAG2 - 8)
-        if g == 17:
-            with jax.named_scope("e1"):
-                stage1(0)
-
     for name, stage, w in (
-        ("f1", stage1, 1), ("e2", stage2, 0), ("f2", stage2, 1), ("e3", stage3, 0), ("e4", stage4, 0),
+        ("e1", stage1, 0), ("f1", stage1, 1), ("e2", stage2, 0), ("f2", stage2, 1), ("e3", stage3, 0), ("e4", stage4, 0),
         ("f3", stage3, 1), ("f4", stage4, 1),
     ):
         with jax.named_scope(name):
@@ -368,9 +372,11 @@
             ):
                 remote(whole, whole, s1s, er_sem.at[0, 0], other_core).wait_send()
         for whole, sem in (
-            (drecv, ds_sem), (r2, s2s), (r3, s3s), (r4, s4s), (drecv.at[0, 0, pl.ds(0, 3)], es_sem)
+            (r2, s2s), (r3, s3s), (r4, s4s), (r2.at[0, 0, pl.ds(0, 3)], es_sem)
         ):
             remote(whole, whole, sem, er_sem.at[0, 0], other_core).wait_send()
+        for g in range(12, 16):
+            d2d(g).wait_send()
 
 
 def local(activations, key_cotangent, value_cotangent):
@@ -389,8 +395,8 @@
             pltpu.VMEM((2, 2, 2, tok, 128), jnp.bfloat16),
             pltpu.VMEM((2, 2, 256, tok), jnp.bfloat16),
             pltpu.VMEM((2, 8, 2, 4, 128, 128), F32),
-            pltpu.VMEM((16, 2, 4, 128, 128), F32),
-            pltpu.VMEM((16, 2, 4, 128, 128), F32),
+            pltpu.VMEM((4, 2, 4, 128, 128), F32),
+            pltpu.VMEM((4, 2, 4, 128, 128), F32),
             pltpu.VMEM((2, 8, 4, 128, 128), F32),
             pltpu.VMEM((2, 8, 2, 2, y_rows, 128), F32),
             pltpu.VMEM((2, 4, 4, 128, 128), F32),
@@ -399,13 +405,13 @@
             pltpu.VMEM((2, 3, 128, 128), F32),
             pltpu.VMEM((2, 128, 128), F32),
             pltpu.VMEM((2, rows, half), F32),
-            dma((8,)), dma((2,)), dma, dma((4,)),
+            dma((8,)), dma((2,)), dma((4,)), dma((4,)),
             dma, dma((2, 28)), dma, dma((2, 6)),
             dma, dma((2, 6)), dma, dma((2, 6)),
             dma, dma((2, 3)),
         ],
         compiler_params=pltpu.CompilerParams(
-            collective_id=0, has_side_effects=True, vmem_limit_bytes=67_043_328
+            collective_id=0, has_side_effects=True, vmem_limit_bytes=LIMIT
         ),
         name="weight_gradients",
     )(activations, key_cotangent, value_cotangent)

time: 64.2 us -> 59.7 us (0.930)
  Pallas kernels: 61.8 us -> 58.2 us
  local copies, waits for them, and re-layouts: 1.69 us -> 0.72 us
    pallas_call x1, Pallas kernels: 61.8 us -> 58.2 us  [local(): pl.pallas_call(kernel, out_shape=jax.ShapeDtypeStruct((2, rows, half), F3...]
    squeeze x1, local copies, waits for them, and re-layouts: 1.69 us -> 0.72 us  [local(): return (both[0], both[1])]
where the time goes in v4:
time: 59.7 us; the launch traced here: 59.6 us
  Pallas kernels  58.2 us (97%)
  local copies, waits for them, and re-layouts  0.72 us (1%)
  between operations  0.64 us (1%)
    pallas_call x1, Pallas kernels, local(): pl.pallas_call(kernel, out_shape=jax.ShapeDtypeStruct((2, rows, half), F3...  58.2 us

profile of v4, /device:TPU:1, one launch (start us, length us, event | category | flops | bytes accessed | tf_op | source)
XLA Modules:
  0.0 59.6 jit_solution(1507180289924371969)
XLA Ops:
  0.6 58.2 %weight_gradients.1 = f32[2,64,512]{2,1,0:T(8,128)S(1)} custom-call(bf16[2048,4096]{1,0:T(8,128)(2,1)} %a_hbm.1, bf16[2048,512]{1,0:T(8,128)(2,1)} %k_hbm.1, bf16[2048,512]{1,0:T(8,128)(2,1)} %v_hbm.1), custom_call_target="tpu_custom_call" | custom-call | tf_op jit(solution)/shard_map/weight_gradients/pallas_call | solution.py:388
  58.8 0.7 %slice_bitcast_fusion = (f32[64,512]{1,0:T(8,128)}, f32[64,512]{1,0:T(8,128)}) fusion(f32[2,64,512]{2,1,0:T(8,128)S(1)} %weight_gradients.1), kind=kLoop, calls=%fused_computation | loop fusion | bytes 524288 | tf_op jit(solution)/shard_map/squeeze | solution.py:418

commit v5 on v4

--- a/solution.py
+++ b/solution.py
@@ -151,6 +151,35 @@
             sem = first_sem(c, w, xt + zt * (2 - xt))
         return remote(acc.at[w, t, n, :, rows], r1.at[w, item, :, rows], s1s, sem, device)
 
+    def direct(c, w, t):
+        index, _, _, _, rows = c
+        for k in (2, 1, 3):
+            src = acc.at[w, t, :, ORDER.index(k), rows]
+            if k == 2:
+                dst, send, sem = r2.at[w, t // 2, pl.ds(t % 2 * 2, 2), rows], s2s, s2r.at[w, index]
+            else:
+                dst, send, sem = r1y.at[w, t, :, k // 2, rows], s1s, first_sem(c, w, t)
+            remote(src, dst, send, sem, peer("y", k)).start()
+
+    def begin(w, t):
+        ys, rest = colours(w)[0:2], colours(w)[2:6]
+        for c in rest:
+            send1(c, w, t).start()
+        if w == 0:
+            for c in ys:
+                send1(c, w, t).start()
+        else:
+
+            @pl.when(t // 4 == 0)
+            def _():
+                for c in ys:
+                    send1(c, w, t).start()
+
+            @pl.when(t // 4 == 1)
+            def _():
+                for c in ys:
+                    direct(c, w, t)
+
     def wait_for(ref, sem):
         remote(ref, ref, s1s, sem, other_core).wait_recv()
 
@@ -188,10 +217,9 @@
 
             @pl.when(g // 8 == wave)
             def _(wave=wave):
-                for c in colours(wave):
-                    send1(c, wave, g % 8).start()
-
-    def second(w, t):
+                begin(wave, g % 8)
+
+    def second(w, t, axes="yxz"):
         xt, zt, m = t // 4, t // 2 % 2, t % 2
 
         def onward(c, n, item):
@@ -200,35 +228,40 @@
             send2(c, w, t, n, item).start()
 
         ys, xs, zs = colours(w)[0:2], colours(w)[2:4], colours(w)[4:6]
-        for c in ys:
-            _, _, p1, p2, rows = c
-            on = ORDER.index(p2)
-            send1(c, w, t).wait_recv()
-            for n in (0, 1):
-                acc[w, t, n, on, rows] = acc[w, t, n, on, rows] + r1y[w, t, n, onward_item(p1), rows]
-            send2(c, w, t, 0, 0).start()
-
-        @pl.when(t == 4)
-        def _():
-            for c in xs:
-                wait_for(r1.at[w, pl.ds(0, 4), :, c[4]], first_sem(c, w, 0))
-
-        @pl.when((zt == 1) & (m == 0))
-        def _():
-            for c in zs:
-                wait_for(r1.at[w, pl.ds(0, 2), :, c[4]], first_sem(c, w, xt))
-
-        @pl.when(xt == 1)
-        def _():
-            for c in xs:
-                n = 1 if c[2] == 1 else 0
-                onward(c, n, zt * 2 + (n + m) % 2)
-
-        @pl.when(zt == 1)
-        def _():
-            for c in zs:
-                n = 1 - m if c[2] == 1 else m
-                onward(c, n, xt * 2 + n)
+        if "y" in axes:
+            for c in ys:
+                _, _, p1, p2, rows = c
+                on = ORDER.index(p2)
+                send1(c, w, t).wait_recv()
+                for n in (0, 1):
+                    acc[w, t, n, on, rows] = acc[w, t, n, on, rows] + r1y[w, t, n, onward_item(p1), rows]
+                send2(c, w, t, 0, 0).start()
+
+        if "x" in axes:
+
+            @pl.when(t == 4)
+            def _():
+                for c in xs:
+                    wait_for(r1.at[w, pl.ds(0, 4), :, c[4]], first_sem(c, w, 0))
+
+            @pl.when(xt == 1)
+            def _():
+                for c in xs:
+                    n = 1 if c[2] == 1 else 0
+                    onward(c, n, zt * 2 + (n + m) % 2)
+
+        if "z" in axes:
+
+            @pl.when((zt == 1) & (m == 0))
+            def _():
+                for c in zs:
+                    wait_for(r1.at[w, pl.ds(0, 2), :, c[4]], first_sem(c, w, xt))
+
+            @pl.when(zt == 1)
+            def _():
+                for c in zs:
+                    n = 1 - m if c[2] == 1 else m
+                    onward(c, n, xt * 2 + n)
 
     def stage1(w):
         for c in colours(w)[2:6]:
@@ -246,11 +279,16 @@
             spread2(c, w)
         for c in colours(w)[0:2]:
             index, _, p1, _, rows = c
+            if w == 1:
+                for t in range(4, 8):
+                    send1(c, w, t).wait_recv()
             wait_for(r2.at[w, :, :, rows], s2r.at[w, index])
             for sx in range(4):
                 for sz in range(4):
                     t, n = unit_at(sx, sz)
                     total = acc[w, t, n, KEEP, rows] + (r1y[w, t, n, kept_item(p1), rows] + r2[w, t // 2, t % 2 * 2 + n, rows])
+                    if w == 1 and t >= 4:
+                        total = total + r1y[w, t, n, onward_item(p1), rows]
                     b2[w, ORDER.index(UNIT_ORDER[sz]), ORDER.index(UNIT_ORDER[sx]), rows] = total
             spread2(c, w)
 
@@ -341,15 +379,18 @@
 
     lax.fori_loop(LAG1, 16, step, 0)
 
-    for g in range(16, 16 + LAG2):
-        if g < 16 + LAG1:
-            with jax.named_scope("own"):
-                d2d(g - LAG1).wait_recv()
-                own(g - LAG1)
-                for c in colours(1):
-                    send1(c, 1, g - LAG1 - 8).start()
-        with jax.named_scope("second"):
-            second(1, g - LAG2 - 8)
+    for g in range(16, 16 + LAG1):
+        with jax.named_scope("own"):
+            d2d(g - LAG1).wait_recv()
+            own(g - LAG1)
+            begin(1, g - LAG1 - 8)
+    left = range(8 - LAG2, 8)
+    with jax.named_scope("second"):
+        for t in left:
+            second(1, t, "x")
+        for t in left:
+            second(1, t, "yz" if t < 4 else "z")
+
     for name, stage, w in (
         ("e1", stage1, 0), ("f1", stage1, 1), ("e2", stage2, 0), ("f2", stage2, 1), ("e3", stage3, 0), ("e4", stage4, 0),
         ("f3", stage3, 1), ("f4", stage4, 1),

time: 59.7 us -> 59.4 us (level)
  no operation moved by 1% of the time
where the time goes in v5:
time: 59.4 us; the launch traced here: 59.3 us
  Pallas kernels  58 us (98%)
  local copies, waits for them, and re-layouts  0.72 us (1%)
  between operations  0.64 us (1%)
    pallas_call x1, Pallas kernels, local(): pl.pallas_call(kernel, out_shape=jax.ShapeDtypeStruct((2, rows, half), F3...  58 us

profile of v5, /device:TPU:1, one launch (start us, length us, event | category | flops | bytes accessed | tf_op | source)
XLA Modules:
  0.0 59.3 jit_solution(1775322074803432282)
XLA Ops:
  0.6 58.0 %weight_gradients.1 = f32[2,64,512]{2,1,0:T(8,128)S(1)} custom-call(bf16[2048,4096]{1,0:T(8,128)(2,1)} %a_hbm.1, bf16[2048,512]{1,0:T(8,128)(2,1)} %k_hbm.1, bf16[2048,512]{1,0:T(8,128)(2,1)} %v_hbm.1), custom_call_target="tpu_custom_call" | custom-call | tf_op jit(solution)/shard_map/weight_gradients/pallas_call | solution.py:429
  58.6 0.7 %slice_bitcast_fusion = (f32[64,512]{1,0:T(8,128)}, f32[64,512]{1,0:T(8,128)}) fusion(f32[2,64,512]{2,1,0:T(8,128)S(1)} %weight_gradients.1), kind=kLoop, calls=%fused_computation | loop fusion | bytes 524288 | tf_op jit(solution)/shard_map/squeeze | solution.py:459
